TPU v7x, 32 devices: a whole 2x2x4 slice. The times are simulated.
32 devices in a mesh: dp: 8 (over z, y), mp: 4 (over x, core).
Axes of the slice: x: 2, y: 2, z: 4, core: 2. Of those that a mesh axis runs over, the one named last changes fastest.
Arguments:
- logits: bfloat16 [1024, 16384], P('dp', 'mp'), may hold values from -72 to 240
- targets: int32 [1024], P('dp'), may hold values from 0 to 16383
- resp_mask: int32 [1024], P('dp'), may hold values from 0 to 1, as said below
- rewards: int32 [8], P('dp'), may hold values from 0 to 10
- groups: int32 [8], P('dp'), may hold values from 0 to 1, as said below
- unit_grad: bfloat16 [1024, 8192], P(('dp', 'mp')), may hold values from -192 to 192
- mix: bfloat16 [1024, 2048], P('dp', 'mp'), may hold values from -6 to 6
- w_out: bfloat16 [2048, 8192], P('mp', 'dp'), may hold values from -0.125 to 0.125
Outputs:
- token_logprob: float32 [1024], P('dp')
- policy_loss: float32 [], replicated
- grad_mix: bfloat16 [1024, 2048], P('dp', 'mp')
- grad_w_out: bfloat16 [2048, 8192], P('mp', 'dp')
Inputs may be any that keep to these rules, and one draw needn't show every extreme that they name: `resp_mask`: in each sample the response mask is a run of ones followed by zeros, with at least 32 ones. `groups`: each prompt id names exactly 4 samples.
All inputs are finite; a program needn't handle non-finite values.
Results may differ from a plain program's by a relative error of at most 0.005.
Values may be sent and summed in bfloat16 or wider, within the bound.
A program may use at most 64 MiB of HBM per device.

v0:
```python
import jax
import jax.numpy as jnp
from jax import lax
from jax.sharding import PartitionSpec as P

K = 4


def shards(logits, targets, resp_mask, rewards, groups, unit_grad, mix, w_out):
    tok_rows, vocab_dev = logits.shape
    mp_lane = lax.axis_index("mp")
    local_target = targets - mp_lane * vocab_dev
    present = (local_target >= 0) & (local_target < vocab_dev)
    picked = jnp.take_along_axis(logits, jnp.clip(local_target, 0, vocab_dev - 1)[:, None], axis=1)[
        :, 0
    ]
    picked = jnp.where(present, picked.astype(jnp.float32), 0.0)
    local_max = jnp.max(logits, axis=1).astype(jnp.float32)
    highest = lax.pmax(local_max, "mp")
    local_sum = jnp.sum(jnp.exp(logits.astype(jnp.float32) - highest[:, None]), axis=1)
    summed, target_logit = lax.psum((local_sum, picked), "mp")
    logprob = target_logit - (highest + jnp.log(summed))
    mask_float = resp_mask.astype(jnp.float32)
    local_count = jnp.sum(mask_float)
    reward_float = rewards.astype(jnp.float32)
    prompt_slots = jnp.arange(lax.axis_size("dp") // K, dtype=jnp.int32)
    own_slot = (prompt_slots == groups[0]).astype(jnp.float32)
    group_total, token_count = lax.psum((own_slot * reward_float[0], local_count), "dp")
    own_total = jnp.sum(own_slot * group_total)
    advantage = reward_float[0] - (own_total - reward_float[0]) / (K - 1)
    weight = advantage * mask_float / token_count
    policy_loss = lax.psum(-jnp.sum(weight * logprob), "dp")
    sub_rows = unit_grad.shape[0]
    part_weight = lax.dynamic_slice_in_dim(weight, mp_lane * sub_rows, sub_rows)
    grad_local = (-part_weight[:, None] * unit_grad.astype(jnp.float32)).astype(jnp.bfloat16)
    grad_group = lax.all_gather(grad_local, "mp", axis=0, tiled=True)
    grad_mix = lax.dot_general(
        grad_group,
        lax.all_gather(w_out, "dp", axis=1, tiled=True),
        (((1,), (1,)), ((), ())),
        preferred_element_type=jnp.float32,
    ).astype(jnp.bfloat16)
    grad_every = lax.all_to_all(grad_group, "dp", split_axis=1, concat_axis=0, tiled=True)
    grad_w_out = lax.dot_general(
        lax.all_gather(mix, "dp", axis=0, tiled=True),
        grad_every,
        (((0,), (0,)), ((), ())),
        preferred_element_type=jnp.float32,
    ).astype(jnp.bfloat16)
    return (logprob, policy_loss, grad_mix, grad_w_out)


def solution(mesh):
    return jax.shard_map(
        shards,
        mesh=mesh,
        in_specs=(
            P("dp", "mp"),
            P("dp"),
            P("dp"),
            P("dp"),
            P("dp"),
            P(("dp", "mp"), None),
            P("dp", "mp"),
            P("mp", "dp"),
        ),
        out_specs=(P("dp"), P(), P("dp", "mp"), P("mp", "dp")),
        check_vma=False,
    )
```

profile of v0, /device:TPU:0, one launch (start us, length us, event | category | flops | bytes accessed | tf_op | source)
XLA Modules:
  0.0 279.9 jit_solution(4905215738061434298)
XLA Ops:
  7.2 0.0 copy-start.2
  7.2 0.0 copy-start.1
  7.2 0.0 all-gather.4.cloned.1.call-start
  7.2 1.3 convert_reduce_fusion
  9.9 23.8 %all-reduce = (f32[]{:T(128)}, f32[2]{0:T(128)S(1)}) all-reduce(f32[]{:T(128)} %convert_reduce_fusion, f32[2]{0:T(128)S(1)} %compare_select_fusion.2), channel_id=1, replica_groups=mesh['dp'=8,'mp'=4] {'dp'}, use_global_device_ids=true, to_apply=%region_8.9 | all-reduce | flops 3 | bytes 24 | tf_op jit(solution)/shard_map/psum | solution.py:28
  33.6 0.6 fusion.1
  34.9 0.7 fusion.2
  35.6 2.3 gather_fusion
  37.9 0.7 and_select_fusion.1
  38.5 1.4 reduce_max.9
  40.0 5.7 %pmax.7 = f32[128]{0:T(128)S(1)} all-reduce(bf16[128]{0:T(256)(128)(2,1)S(1)} %reduce_max.9), channel_id=1, replica_groups=mesh['dp'=8,'mp'=4] {'mp'}, use_global_device_ids=true, to_apply=%region_2.3 | all-reduce | flops 128 | bytes 768 | tf_op jit(solution)/shard_map/pmax | solution.py:19
  45.6 1.7 exponential_reduce_fusion
  47.4 6.6 %all-reduce.1 = (f32[128]{0:T(128)S(1)}, f32[128]{0:T(128)S(1)}) all-reduce(f32[128]{0:T(128)S(1)} %and_select_fusion.1, f32[128]{0:T(128)S(1)} %exponential_reduce_fusion), channel_id=1, replica_groups=mesh['dp'=8,'mp'=4] {'mp'}, use_global_device_ids=true, to_apply=%region_0.1 | all-reduce | flops 256 | bytes 2048 | tf_op jit(solution)/shard_map/psum | solution.py:21
  53.9 0.0 copy-done.2
  53.9 1.8 multiply_reduce_fusion
  55.7 0.1 dynamic-slice_negate_fusion
  55.8 0.0 copy-done.1
  55.8 0.9 multiply_convert_fusion
  56.7 0.0 all-gather.4.cloned.1.call-update
  56.7 0.0 all-gather.8.cloned.1.call-start
  56.8 0.7 all-gather.8.cloned.1.call-update
  57.5 0.0 all-gather.6.cloned.1.call-start
  57.5 0.7 all-gather.6.cloned.1.call-update
  58.2 18.0 %all-gather.4.cloned.1.call-done = bf16[128,8192]{1,0:T(8,128)(2,1)} async-done(((bf16[32,8192]{1,0:T(8,128)(2,1)}), bf16[128,8192]{1,0:T(8,128)(2,1)}) %all-gather.4.cloned.1.call-update) | async-done | bytes 2097168 | tf_op jit(solution)/shard_map/all_gather | solution.py:36
  76.2 4.1 %copy.17 = bf16[128,8192]{0,1:T(8,128)(2,1)} copy(bf16[128,8192]{1,0:T(8,128)(2,1)} %all-gather.4.cloned.1.call-done) | data formatting | bytes 4194304 | tf_op jit(solution)/shard_map/all_gather | solution.py:36
  80.3 5.5 %all-to-all-start = ((bf16[128,8,1024]{0,2,1:T(8,128)(2,1)}), bf16[128,8,1024]{0,2,1:T(8,128)(2,1)S(1)}, u32[]{:S(2)}, u32[]{:S(2)}) async-start(bf16[128,8,1024]{0,2,1:T(8,128)(2,1)} %bitcast.20), calls=%async_computation | async-start | bytes 4194304 | tf_op jit(solution)/shard_map/all_to_all | solution.py:43
  86.4 56.0 %psum.39 = f32[]{:T(128)} all-reduce(f32[]{:T(128)S(6)} %neg.7), channel_id=1, replica_groups=mesh['dp'=8,'mp'=4] {'dp'}, use_global_device_ids=true, to_apply=%region_10.11 | all-reduce | flops 1 | bytes 8 | tf_op jit(solution)/shard_map/psum | solution.py:32
  142.5 4.6 %all-to-all-done = bf16[128,8,1024]{0,2,1:T(8,128)(2,1)S(1)} async-done(((bf16[128,8,1024]{0,2,1:T(8,128)(2,1)}), bf16[128,8,1024]{0,2,1:T(8,128)(2,1)S(1)}, u32[]{:S(2)}, u32[]{:S(2)}) %all-to-all-start) | async-done | bytes 2097184 | tf_op jit(solution)/shard_map/all_to_all | solution.py:43
  147.1 2.6 copy.18
  149.7 0.0 all-gather.8.cloned.1.call-done
  149.7 3.4 %fusion = bf16[512,1024]{0,1:T(8,128)(2,1)S(1)} fusion(bf16[1024,1024]{1,0:T(8,128)(2,1)} %bitcast.21, bf16[1024,512]{1,0:T(8,128)(2,1)} %all-gather.8.cloned.1.call-done), kind=kOutput, calls=%fused_computation.3 | convolution fusion | flops 1074266112 | bytes 4194304 | tf_op jit(solution)/shard_map/dot_general | solution.py:44
  153.1 0.0 copy-start
  153.1 1.3 copy.19
  154.4 112.0 %all-gather.6.cloned.1.call-done = bf16[512,8192]{1,0:T(8,128)(2,1)} async-done(((bf16[512,1024]{1,0:T(8,128)(2,1)}), bf16[512,8192]{1,0:T(8,128)(2,1)}) %all-gather.6.cloned.1.call-update) | async-done | bytes 8388624 | tf_op jit(solution)/shard_map/all_gather | solution.py:39
  266.4 0.0 copy-done
  266.4 7.0 %convolution_convert_fusion.1 = bf16[128,512]{1,0:T(8,128)(2,1)} fusion(bf16[128,8192]{1,0:T(8,128)(2,1)S(1)} %copy-done, bf16[512,8192]{1,0:T(8,128)(2,1)} %all-gather.6.cloned.1.call-done), kind=kOutput, calls=%fused_computation.4 | convolution fusion | flops 1073807360 | bytes 10616832 | tf_op jit(solution)/shard_map/dot_general | solution.py:37
  (4 shorter events, 0.0 us)
Async XLA Ops:
  7.2 46.8 %copy-start.2 = (s32[128]{0:T(128)S(1)}, s32[128]{0:T(128)}, u32[]{:S(2)}) copy-start(s32[128]{0:T(128)} %param.10) | copy-start | bytes 1540
  7.2 48.6 %copy-start.1 = (bf16[32,8192]{1,0:T(8,128)(2,1)S(1)}, bf16[32,8192]{1,0:T(8,128)(2,1)}, u32[]{:S(2)}) copy-start(bf16[32,8192]{1,0:T(8,128)(2,1)} %param.13) | copy-start | bytes 1572868
  7.2 69.0 %all-gather.4.cloned.1.call-start = ((), (), s32[]{:S(2)}) async-start(), calls=%async_computation.1 | async-start | bytes 2621440 | tf_op jit(solution)/shard_map/all_gather | solution.py:36
  56.7 92.9 %all-gather.8.cloned.1.call-start = ((), (), s32[]{:S(2)}) async-start(), calls=%async_computation.3 | async-start | bytes 1179648 | tf_op jit(solution)/shard_map/all_gather | solution.py:45
  57.5 208.9 %all-gather.6.cloned.1.call-start = ((), (), s32[]{:S(2)}) async-start(), calls=%async_computation.2 | async-start | bytes 9437184 | tf_op jit(solution)/shard_map/all_gather | solution.py:39
  80.3 66.8 %all-to-all-start = ((bf16[128,8,1024]{0,2,1:T(8,128)(2,1)}), bf16[128,8,1024]{0,2,1:T(8,128)(2,1)S(1)}, u32[]{:S(2)}, u32[]{:S(2)}) async-start(bf16[128,8,1024]{0,2,1:T(8,128)(2,1)} %bitcast.20), calls=%async_computation | async-start | bytes 4194304 | tf_op jit(solution)/shard_map/all_to_all | solution.py:43
  153.1 113.3 %copy-start = (bf16[128,8192]{1,0:T(8,128)(2,1)S(1)}, bf16[128,8192]{1,0:T(8,128)(2,1)}, u32[]{:S(2)}) copy-start(bf16[128,8192]{1,0:T(8,128)(2,1)} %all-gather.4.cloned.1.call-done) | copy-start | bytes 6291460
Sparse Core Ops, SparseCore 0:
  56.9 19.2 all-gather.3
  78.3 63.1 all-gather.7
  143.7 122.6 all-gather.5
where the time goes:
time: 280 us
  waiting for transfers between devices  136 us (49%)
  blocking collectives  92 us (33%)
  between operations  16.4 us (6%)
  matrix products  10.4 us (4%)
  local copies, waits for them, and re-layouts  10.3 us (4%)
  other arithmetic  9.22 us (3%)
  starting transfers between devices  5.63 us (2%)
    all_gather x1, waiting for transfers between devices, shards(): lax.all_gather(w_out, 'dp', axis=1, tiled=True)  112 us
    psum x1, blocking collectives, shards(): policy_loss = lax.psum(-jnp.sum(weight * logprob), 'dp')  56 us
    psum x1, blocking collectives, shards(): lax.psum((own_slot * reward_float[0], local_count), 'dp')  23.8 us
    all_gather x1, waiting for transfers between devices, shards(): grad_group = lax.all_gather(grad_local, 'mp', axis=0, tiled=True)  18 us
    dot_general x1, matrix products, shards(): lax.dot_general(grad_group, lax.all_gather(w_out, 'dp', axis=1, tiled=Tru...  6.96 us
    psum x1, blocking collectives, shards(): summed, target_logit = lax.psum((local_sum, picked), 'mp')  6.56 us
    pmax x1, blocking collectives, shards(): highest = lax.pmax(local_max, 'mp')  5.66 us
  transfers between devices with their start and end apart: 4, of which 3 were waited for; matrix products, arithmetic and copies ran while one was open for 4% of the time, Pallas kernels for 0%

commit v1 on v0

--- a/solution.py
+++ b/solution.py
@@ -33,7 +33,9 @@
     sub_rows = unit_grad.shape[0]
     part_weight = lax.dynamic_slice_in_dim(weight, mp_lane * sub_rows, sub_rows)
     grad_local = (-part_weight[:, None] * unit_grad.astype(jnp.float32)).astype(jnp.bfloat16)
-    grad_group = lax.all_gather(grad_local, "mp", axis=0, tiled=True)
+    grad_group = jnp.concatenate(
+        lax.all_to_all(jnp.stack([grad_local] * lax.axis_size("mp")), "mp", 0, 0), axis=0
+    )
     grad_mix = lax.dot_general(
         grad_group,
         lax.all_gather(w_out, "dp", axis=1, tiled=True),

time: 280 us -> 228 us (0.81)
  waiting for transfers between devices: 136 us -> 49.3 us
  blocking collectives: 92 us -> 134 us
  other arithmetic: 9.22 us -> 5.28 us
    all_gather x1, waiting for transfers between devices: 112 us -> 30.5 us  [shards(): lax.all_gather(w_out, 'dp', axis=1, tiled=True)]
    all_to_all x0 -> x1, blocking collectives: none -> 28.1 us  [shards(): lax.all_to_all(jnp.stack([grad_local] * lax.axis_size('mp')), 'mp', 0, 0)]
    all_gather x1 -> x0, waiting for transfers between devices: 18 us -> none  [shards(): grad_group = lax.all_gather(grad_local, 'mp', axis=0, tiled=True)]
    psum x1, blocking collectives: 56 us -> 69.7 us  [shards(): policy_loss = lax.psum(-jnp.sum(weight * logprob), 'dp')]
    all_to_all x1, waiting for transfers between devices: 4.61 us -> 17.5 us  [shards(): lax.all_to_all(grad_group, 'dp', split_axis=1, concat_axis=0, tiled=True)]
    all_gather x1 -> x0, local copies, waits for them, and re-layouts: 4.07 us -> none  [shards(): grad_group = lax.all_gather(grad_local, 'mp', axis=0, tiled=True)]
  transfers between devices with their start and end apart: 4 -> 3, of which waited for: 3 -> 2; matrix products, arithmetic and copies ran while one was open for 4% -> 7% of each run, Pallas kernels for 0% -> 0%
where the time goes in v1:
time: 228 us
  blocking collectives  134 us (59%)
  waiting for transfers between devices  49.3 us (22%)
  between operations  16.7 us (7%)
  matrix products  10.1 us (4%)
  local copies, waits for them, and re-layouts  7.66 us (3%)
  other arithmetic  5.28 us (2%)
  starting transfers between devices  4.43 us (2%)
    psum x1, blocking collectives, shards(): policy_loss = lax.psum(-jnp.sum(weight * logprob), 'dp')  69.7 us
    all_gather x1, waiting for transfers between devices, shards(): lax.all_gather(w_out, 'dp', axis=1, tiled=True)  30.5 us
    all_to_all x1, blocking collectives, shards(): lax.all_to_all(jnp.stack([grad_local] * lax.axis_size('mp')), 'mp', 0, 0)  28.1 us
    psum x1, blocking collectives, shards(): lax.psum((own_slot * reward_float[0], local_count), 'dp')  23.8 us
    all_to_all x1, waiting for transfers between devices, shards(): lax.all_to_all(grad_group, 'dp', split_axis=1, concat_axis=0, tiled=True)  17.5 us
    dot_general x1, matrix products, shards(): lax.dot_general(grad_group, lax.all_gather(w_out, 'dp', axis=1, tiled=Tru...  6.96 us
    psum x1, blocking collectives, shards(): summed, target_logit = lax.psum((local_sum, picked), 'mp')  6.57 us
    pmax x1, blocking collectives, shards(): highest = lax.pmax(local_max, 'mp')  6.07 us
  transfers between devices with their start and end apart: 3, of which 2 were waited for; matrix products, arithmetic and copies ran while one was open for 7% of the time, Pallas kernels for 0%

profile of v1, /device:TPU:0, one launch (start us, length us, event | category | flops | bytes accessed | tf_op | source)
XLA Modules:
  0.0 227.8 jit_solution(18152395308843807440)
XLA Ops:
  7.2 0.0 copy-start.2
  7.2 0.0 copy-start.3
  7.2 0.0 copy-start
  7.2 0.0 copy-start.1
  7.2 0.0 all-gather.5.cloned.1.call-start
  7.3 0.7 all-gather.5.cloned.1.call-update
  7.9 0.0 all-gather.3.cloned.1.call-start
  8.0 0.7 all-gather.3.cloned.1.call-update
  10.0 1.3 convert_reduce_fusion
  11.3 23.8 %all-reduce = (f32[]{:T(128)}, f32[2]{0:T(128)S(1)}) all-reduce(f32[]{:T(128)} %convert_reduce_fusion, f32[2]{0:T(128)S(1)} %compare_select_fusion.2), channel_id=1, replica_groups=mesh['dp'=8,'mp'=4] {'dp'}, use_global_device_ids=true, to_apply=%region_8.9 | all-reduce | flops 3 | bytes 24 | tf_op jit(solution)/shard_map/psum | solution.py:28
  35.1 0.6 fusion.1
  36.3 0.7 fusion.2
  37.0 2.3 gather_fusion
  39.3 0.0 copy-done
  39.3 0.2 reduce_max.9
  39.5 6.1 %pmax.7 = f32[128]{0:T(128)S(1)} all-reduce(bf16[128]{0:T(256)(128)(2,1)S(1)} %reduce_max.9), channel_id=1, replica_groups=mesh['dp'=8,'mp'=4] {'mp'}, use_global_device_ids=true, to_apply=%region_2.3 | all-reduce | flops 128 | bytes 768 | tf_op jit(solution)/shard_map/pmax | solution.py:19
  45.6 0.5 exponential_reduce_fusion
  46.1 0.0 copy-done.3
  46.1 6.6 %all-reduce.1 = (f32[128]{0:T(128)S(1)}, f32[128]{0:T(128)S(1)}) all-reduce(f32[128]{0:T(128)S(1)} %and_select_fusion.1, f32[128]{0:T(128)S(1)} %exponential_reduce_fusion), channel_id=1, replica_groups=mesh['dp'=8,'mp'=4] {'mp'}, use_global_device_ids=true, to_apply=%region_0.1 | all-reduce | flops 256 | bytes 2048 | tf_op jit(solution)/shard_map/psum | solution.py:21
  52.7 0.0 copy-done.2
  52.7 1.8 multiply_reduce_fusion
  54.4 0.1 dynamic-slice_negate_fusion
  54.5 0.0 copy-done.1
  54.5 0.2 multiply_convert_fusion
  54.7 0.2 stack.2
  54.9 28.1 %all_to_all.24 = bf16[4,32,8192]{2,1,0:T(8,128)(2,1)S(1)} all-to-all(bf16[4,32,8192]{2,1,0:T(8,128)(2,1)S(1)} %stack.2), channel_id=1, replica_groups=mesh['dp'=8,'mp'=4] {'mp'}, dimensions={0} | all-to-all | bytes 4194304 | tf_op jit(solution)/shard_map/all_to_all | solution.py:37
  83.0 1.4 copy.18
  84.4 2.4 %copy.16 = bf16[128,8,1024]{2,0,1:T(8,128)(2,1)} copy(bf16[128,8,1024]{2,1,0:T(8,128)(2,1)S(1)} %bitcast.25) | data formatting | bytes 4194304 | tf_op jit(solution)/shard_map/all_to_all | solution.py:45
  86.9 4.4 %all-to-all-start.1 = ((bf16[128,8,1024]{2,0,1:T(8,128)(2,1)}), bf16[128,8,1024]{2,0,1:T(8,128)(2,1)}, u32[]{:S(2)}, u32[]{:S(2)}) async-start(bf16[128,8,1024]{2,0,1:T(8,128)(2,1)} %copy.16), calls=%async_computation.1 | async-start | bytes 4194304 | tf_op jit(solution)/shard_map/all_to_all | solution.py:45
  91.9 69.7 %psum.39 = f32[]{:T(128)} all-reduce(f32[]{:T(128)S(6)} %neg.7), channel_id=1, replica_groups=mesh['dp'=8,'mp'=4] {'dp'}, use_global_device_ids=true, to_apply=%region_10.11 | all-reduce | flops 1 | bytes 8 | tf_op jit(solution)/shard_map/psum | solution.py:32
  161.6 0.0 all-gather.5.cloned.1.call-done
  161.6 17.5 %all-to-all-done.1 = bf16[128,8,1024]{2,0,1:T(8,128)(2,1)} async-done(((bf16[128,8,1024]{2,0,1:T(8,128)(2,1)}), bf16[128,8,1024]{2,0,1:T(8,128)(2,1)}, u32[]{:S(2)}, u32[]{:S(2)}) %all-to-all-start.1) | async-done | bytes 2097184 | tf_op jit(solution)/shard_map/all_to_all | solution.py:45
  179.1 3.1 %fusion = bf16[512,1024]{0,1:T(8,128)(2,1)S(1)} fusion(bf16[1024,1024]{1,0:T(8,128)(2,1)} %bitcast.7, bf16[1024,512]{1,0:T(8,128)(2,1)} %all-gather.5.cloned.1.call-done), kind=kOutput, calls=%fused_computation.3 | convolution fusion | flops 1074266112 | bytes 4194304 | tf_op jit(solution)/shard_map/dot_general | solution.py:46
  182.2 1.3 copy.17
  183.5 30.5 %all-gather.3.cloned.1.call-done = bf16[512,8192]{1,0:T(8,128)(2,1)} async-done(((bf16[512,1024]{1,0:T(8,128)(2,1)}), bf16[512,8192]{1,0:T(8,128)(2,1)}) %all-gather.3.cloned.1.call-update) | async-done | bytes 8388624 | tf_op jit(solution)/shard_map/all_gather | solution.py:41
  214.0 7.0 %convolution_convert_fusion.1 = bf16[128,512]{1,0:T(8,128)(2,1)} fusion(bf16[128,8192]{1,0:T(8,128)(2,1)S(1)} %bitcast.24, bf16[512,8192]{1,0:T(8,128)(2,1)} %all-gather.3.cloned.1.call-done), kind=kOutput, calls=%fused_computation.4 | convolution fusion | flops 1073807360 | bytes 10616832 | tf_op jit(solution)/shard_map/dot_general | solution.py:39
  (5 shorter events, 0.0 us)
Async XLA Ops:
  7.2 45.5 %copy-start.2 = (s32[128]{0:T(128)S(1)}, s32[128]{0:T(128)}, u32[]{:S(2)}) copy-start(s32[128]{0:T(128)} %param.10) | copy-start | bytes 1540
  7.2 38.9 %copy-start.3 = (s32[128]{0:T(128)S(1)}, s32[128]{0:T(128)}, u32[]{:S(2)}) copy-start(s32[128]{0:T(128)} %param.9) | copy-start | bytes 1540
  7.2 32.1 %copy-start = (bf16[128,4096]{1,0:T(8,128)(2,1)S(1)}, bf16[128,4096]{1,0:T(8,128)(2,1)}, u32[]{:S(2)}) copy-start(bf16[128,4096]{1,0:T(8,128)(2,1)} %param.8) | copy-start | bytes 3145732
  7.2 47.3 %copy-start.1 = (bf16[32,8192]{1,0:T(8,128)(2,1)S(1)}, bf16[32,8192]{1,0:T(8,128)(2,1)}, u32[]{:S(2)}) copy-start(bf16[32,8192]{1,0:T(8,128)(2,1)} %param.13) | copy-start | bytes 1572868
  7.2 154.4 %all-gather.5.cloned.1.call-start = ((), (), s32[]{:S(2)}) async-start(), calls=%async_computation.3 | async-start | bytes 1179648 | tf_op jit(solution)/shard_map/all_gather | solution.py:47
  7.9 206.1 %all-gather.3.cloned.1.call-start = ((), (), s32[]{:S(2)}) async-start(), calls=%async_computation.2 | async-start | bytes 9437184 | tf_op jit(solution)/shard_map/all_gather | solution.py:41
  86.9 92.2 %all-to-all-start.1 = ((bf16[128,8,1024]{2,0,1:T(8,128)(2,1)}), bf16[128,8,1024]{2,0,1:T(8,128)(2,1)}, u32[]{:S(2)}, u32[]{:S(2)}) async-start(bf16[128,8,1024]{2,0,1:T(8,128)(2,1)} %copy.16), calls=%async_computation.1 | async-start | bytes 4194304 | tf_op jit(solution)/shard_map/all_to_all | solution.py:45
Sparse Core Ops, SparseCore 0:
  10.1 43.0 all-gather.4
  55.4 158.5 all-gather.2
